TPU v7x, 32 devices: a whole 2x2x4 slice. The times are simulated.
32 devices in a mesh: ka: 8 (over z, x), row: 4 (over y, core).
Axes of the slice: x: 2, y: 2, z: 4, core: 2. Of those that a mesh axis runs over, the one named last changes fastest.
Arguments:
- gauge: bfloat16 [32, 2, 384, 384], P(('ka', 'row')), may hold values from -3 to 3
- energies: float32 [32, 384], P(('ka', 'row')), may hold values from -5 to 5
- kmesh: int32 [3, 32], replicated, may hold values from 0 to 11
- lattice: int32 [3, 256], P(None, 'row'), may hold values from -8 to 8
- degeneracy: int32 [256], P('row'), may hold values from 1 to 8
- path: int32 [3, 8], replicated, may hold values from 0 to 63
Outputs:
- lattice_h: bfloat16 [256, 384, 768], P('row', 'ka')
- path_h: float32 [8, 384, 768], P('row', 'ka')
All inputs are finite; a program needn't handle non-finite values.
Results may differ from a plain program's by a relative error of at most 0.006.
Values may be sent and summed in bfloat16 or wider, within the bound.
No kernel may reach another device: no remote copies, remote signals or barrier semaphores. Data moves between devices by JAX's collectives and lax.ppermute only.
A program may use at most 64 MiB of HBM per device.

v0:
```python
import math
import jax
import jax.numpy as jnp
from jax import lax
from jax.sharding import PartitionSpec as P

MESH = 12
PATH_DEN = 64


def phases(vectors, coords):
    windings = jnp.mod(jnp.sum(vectors[:, :, None] * coords[:, None, :], 0), MESH)
    angles = windings.astype(jnp.float32) * (2.0 * math.pi / MESH)
    return jnp.concatenate([jnp.cos(angles), jnp.sin(angles)], 0).astype(jnp.bfloat16)


def path_factors(path_coords, vectors, counts):
    windings = jnp.mod(jnp.sum(path_coords[:, :, None] * vectors[:, None, :], 0), PATH_DEN)
    angles = windings.astype(jnp.float32) * (2.0 * math.pi / PATH_DEN)
    weights = 1.0 / counts.astype(jnp.float32)
    return jnp.concatenate(
        [jnp.cos(angles) * weights[None, :], jnp.sin(angles) * weights[None, :]], 0
    ).astype(jnp.bfloat16)


def combine_fourier(products, scale_by):
    real_part = products[0, :, :, 0] + products[1, :, :, 1]
    imag_part = products[0, :, :, 1] - products[1, :, :, 0]
    return jnp.concatenate([real_part, imag_part], -1) / scale_by


def combine_path(products):
    real_part = products[0, :, :, 0] - products[1, :, :, 1]
    imag_part = products[0, :, :, 1] + products[1, :, :, 0]
    return jnp.concatenate([real_part, imag_part], -1)


def local(gauge, energies, kmesh, lattice, degeneracy, path):
    per_device = gauge.shape[0]
    orbitals = gauge.shape[2]
    ka_count = lax.axis_size("ka")
    row_count = lax.axis_size("row")
    k_total = kmesh.shape[1]
    path_dev = path.shape[1] // row_count
    scaled = (energies[:, None, :, None] * gauge.astype(jnp.float32)).astype(jnp.bfloat16)
    stacked = jnp.concatenate([gauge[:, 0], gauge[:, 1]], 1)
    partner = jnp.concatenate(
        [
            jnp.concatenate([scaled[:, 0], scaled[:, 1]], 2),
            jnp.concatenate([scaled[:, 1], -scaled[:, 0]], 2),
        ],
        1,
    )
    rotated = jnp.einsum(
        "kna,knb->kab", stacked, partner, preferred_element_type=jnp.float32
    ).astype(jnp.bfloat16)
    arrived = lax.all_to_all(rotated, "ka", split_axis=1, concat_axis=0, tiled=True)
    local_rows = arrived.shape[1]
    lattice_rows = lattice.shape[1]
    k_order = (
        kmesh.reshape(3, ka_count, row_count, per_device).transpose(0, 2, 1, 3).reshape(3, k_total)
    )
    vectors_all, counts_all = (
        lax.all_gather(lattice, "row", axis=1, tiled=True),
        lax.all_gather(degeneracy, "row", axis=0, tiled=True),
    )
    total_vectors = vectors_all.shape[1]
    own_path = lax.dynamic_slice_in_dim(path, lax.axis_index("row") * path_dev, path_dev, 1)
    factors_path = path_factors(own_path, vectors_all, counts_all).astype(jnp.float32)
    factors_mesh = phases(vectors_all, k_order).astype(jnp.float32)
    with_cos = jnp.dot(
        factors_path,
        factors_mesh[:total_vectors],
        preferred_element_type=jnp.float32,
        precision=lax.Precision.HIGHEST,
    )
    with_sin = jnp.dot(
        factors_path,
        factors_mesh[total_vectors:],
        preferred_element_type=jnp.float32,
        precision=lax.Precision.HIGHEST,
    )
    mixing_real = (with_cos[:path_dev] + with_sin[path_dev:]) / k_total
    mixing_imag = (with_cos[path_dev:] - with_sin[:path_dev]) / k_total
    mixing = jnp.concatenate([mixing_real, mixing_imag], 0)
    k_piece = lax.all_gather(arrived, "row", axis=0, tiled=True)
    amount = k_piece.shape[0]
    fourier_amount = k_piece.shape[0]
    factors = phases(lattice, k_order)
    fourier_sum = jnp.dot(
        factors, k_piece.reshape(fourier_amount, -1), preferred_element_type=jnp.float32
    )
    path_sum = jnp.dot(
        mixing,
        k_piece.reshape(amount, -1).astype(jnp.float32),
        preferred_element_type=jnp.float32,
        precision=lax.Precision.HIGHEST,
    )
    summed, path_sum = (fourier_sum, path_sum)
    products = summed.reshape(2, lattice_rows, local_rows, 2, orbitals)
    lattice_f = combine_fourier(products, k_total)
    path_h = combine_path(path_sum.reshape(2, path_dev, local_rows, 2, orbitals))
    lattice_h = lattice_f.astype(jnp.bfloat16)
    return (lattice_h, path_h)


def solution(mesh):
    return jax.shard_map(
        local,
        mesh=mesh,
        in_specs=(
            P(("ka", "row"), None, None, None),
            P(("ka", "row"), None),
            P(),
            P(None, "row"),
            P("row"),
            P(),
        ),
        out_specs=(P("row", "ka", None), P("row", "ka", None)),
        check_vma=False,
    )
```

profile of v0, /device:TPU:0, one launch (start us, length us, event | category | flops | bytes accessed | tf_op | source)
XLA Modules:
  0.0 96.4 jit_solution(5764981165644782622)
XLA Ops:
  7.2 0.7 reduce
  7.9 1.2 %multiply_convert_fusion = bf16[1,2,384,384]{3,2,1,0:T(8,128)(2,1)S(1)} fusion(bf16[1,2,384,384]{3,2,1,0:T(8,128)(2,1)} %param.6, f32[384]{0:T(512)S(1)} %reduce), kind=kLoop, calls=%fused_computation.23 | loop fusion | flops 884736 | bytes 1181184 | tf_op jit(solution)/shard_map/convert_element_type | solution.py:45
  9.2 1.3 %slice_bitcast_fusion.3 = (bf16[1,384,384]{2,1,0:T(8,128)(2,1)S(1)}, bf16[1,384,384]{2,1,0:T(8,128)(2,1)S(1)}, bf16[1,384,384]{2,1,0:T(8,128)(2,1)S(1)}, bf16[1,384,384]{2,1,0:T(8,128)(2,1)S(1)}) fusion(bf16[1,2,384,384]{3,2,1,0:T(8,128)(2,1)S(1)} %multiply_convert_fusion, bf16[1,2,384,384]{3,2,1,0:T(8,128)(2,1)} %param.6), kind=kLoop, calls=%fused_computation.28 | loop fusion | bytes 2359296 | tf_op jit(solution)/shard_map/squeeze | solution.py:49
  10.5 0.7 fusion.10
  11.1 0.9 copy.83
  12.0 0.5 broadcast.30
  12.6 4.4 %reduce.1 = bf16[384,768]{1,0:T(8,128)(2,1)S(1)} reduce(bf16[384,1,768]{2,1,0:T(2,128)(2,1)S(1)} %bitcast.83, bf16[]{:T(256)} %broadcast.30), dimensions={1}, to_apply=%bitcast.81.reduce_sub_computation | reduce | bytes 1179650
  17.1 23.6 %all_to_all.12 = bf16[8,2,18432]{2,1,0:T(2,128)(2,1)S(1)} all-to-all(bf16[8,2,18432]{2,1,0:T(2,128)(2,1)S(1)} %reshape.77), channel_id=1, replica_groups=mesh['ka'=8,'row'=4] {'ka'}, dimensions={0} | all-to-all | bytes 1179648 | tf_op jit(solution)/shard_map/all_to_all | solution.py:57
  40.7 0.6 reshape.78
  41.3 0.9 copy.66
  42.2 5.2 %all-gather = s32[4,64,3]{1,2,0:T(4,128)S(1)} all-gather(s32[1,64,3]{1,2,0:T(4,128)S(1)} %bitcast.92), channel_id=1, replica_groups=mesh['ka'=8,'row'=4] {'row'}, dimensions={0}, use_global_device_ids=true | all-gather | bytes 3840 | tf_op jit(solution)/shard_map/all_gather | solution.py:64
  48.1 0.6 dynamic-slice
  49.6 5.2 %all-reduce = s32[256]{0:T(256)S(1)} all-reduce(s32[256]{0:T(256)S(1)} %dynamic-update-slice), channel_id=1, replica_groups=mesh['ka'=8,'row'=4] {'row'}, use_global_device_ids=true, to_apply=%add | all-reduce | flops 256 | bytes 2048
  55.4 0.3 fusion.27
  55.7 9.2 %all-gather.3.cloned.1.call-done = bf16[32,48,768]{2,1,0:T(8,128)(2,1)} async-done(((bf16[8,48,768]{2,1,0:T(8,128)(2,1)}), bf16[32,48,768]{2,1,0:T(8,128)(2,1)}) %all-gather.3.cloned.1.call-update) | async-done | bytes 2359312 | tf_op jit(solution)/shard_map/all_gather | solution.py:86
  64.9 3.8 %copy.71 = bf16[4,8,48,768]{3,1,2,0:T(8,128)(2,1)} copy(bf16[4,8,48,768]{3,2,1,0:T(8,128)(2,1)} %bitcast.86) | data formatting | bytes 4718592
  68.8 3.5 %dot_general.23 = bf16[48,2,384,32]{2,1,0,3:T(2,128)(2,1)S(1)} reshape(bf16[36864,32]{0,1:T(8,128)(2,1)} %bitcast.82) | data formatting | bytes 4718592 | tf_op jit(solution)/shard_map/dot_general | solution.py:90
  72.3 1.5 %fusion.4 = f32[2,2,48,2,384]{4,1,3,2,0:T(2,128)S(1)} fusion(f32[2,2,32,1,1]{2,1,4,3,0:T(2,128)S(1)} %bitcast.91, bf16[48,2,384,32]{2,1,0,3:T(2,128)(2,1)S(1)} %dot_general.23), kind=kOutput, calls=%fused_computation.8 | convolution fusion | flops 56623104 | bytes 2949632 | tf_op jit(solution)/shard_map/dot_general | solution.py:93
  74.0 2.6 %fusion.6 = f32[2,64,48,2,384]{4,1,3,2,0:T(8,128)S(1)} fusion(bf16[48,2,384,32]{2,1,0,3:T(2,128)(2,1)S(1)} %dot_general.23, bf16[2,64,32,1,1]{1,0,2,4,3:T(2,128)(2,1)S(1)} %bitcast.87), kind=kOutput, calls=%fused_computation.10 | convolution fusion | flops 301989888 | bytes 21241856 | tf_op jit(solution)/shard_map/dot_general | solution.py:90
  76.6 0.8 fusion.1
  77.4 0.8 fusion.3
  78.3 0.7 copy.61
  79.1 3.3 %fusion = bf16[64,48,768]{2,0,1:T(8,128)(2,1)} fusion(f32[64,48,384]{2,0,1:T(8,128)S(1)} %fusion.1, f32[64,48,384]{2,0,1:T(8,128)S(1)} %fusion.3), kind=kLoop, calls=%fused_computation.1 | loop fusion | flops 7077888 | bytes 14155776 | tf_op jit(solution)/shard_map/convert_element_type | solution.py:103
  82.4 7.1 %copy.60 = bf16[64,48,768]{2,1,0:T(8,128)(2,1)} copy(bf16[64,48,768]{2,0,1:T(8,128)(2,1)} %fusion) | data formatting | bytes 9437184
  (37 shorter events, 2.1 us)
Async XLA Ops:
  7.2 47.6 %copy-start = (s32[3,8]{1,0:T(4,128)S(1)}, s32[3,8]{1,0:T(4,128)}, u32[]{:S(2)}) copy-start(s32[3,8]{1,0:T(4,128)} %param.11) | copy-start | bytes 292
  7.2 57.8 %all-gather.3.cloned.1.call-start = ((), (), s32[]{:S(2)}) async-start(), calls=%async_computation.1 | async-start | bytes 2949120 | tf_op jit(solution)/shard_map/all_gather | solution.py:86
  40.7 1.5 %copy-start.1 = (s32[3,64]{1,0:T(4,128)S(1)}, s32[3,64]{1,0:T(4,128)}, u32[]{:S(2)}) copy-start(s32[3,64]{1,0:T(4,128)} %param.9) | copy-start | bytes 2308
  40.7 6.8 %copy-start.2 = (s32[3,32]{1,0:T(4,128)S(1)}, s32[3,32]{1,0:T(4,128)}, u32[]{:S(2)}) copy-start(s32[3,32]{1,0:T(4,128)} %param.8) | copy-start | bytes 1156
  40.7 7.4 %copy-start.4 = (u32[32]{0:T(128)S(1)}, u32[32]{0:T(128)}, u32[]{:S(2)}) copy-start(u32[32]{0:T(128)} %constant.58) | copy-start | bytes 388
  40.7 8.7 %copy-start.3 = (s32[64]{0:T(128)S(1)}, s32[64]{0:T(128)}, u32[]{:S(2)}) copy-start(s32[64]{0:T(128)} %param.10) | copy-start | bytes 772
Sparse Core Ops, SparseCore 0:
  42.3 22.5 all-gather.2
where the time goes:
time: 96.8 us; the launch traced here: 96.4 us
  blocking collectives  34 us (35%)
  local copies, waits for them, and re-layouts  20.9 us (22%)
  between operations  14.9 us (15%)
  other arithmetic  12 us (12%)
  waiting for transfers between devices  9.25 us (10%)
  matrix products  5.35 us (6%)
    all_to_all x1, blocking collectives, local(): lax.all_to_all(rotated, 'ka', split_axis=1, concat_axis=0, tiled=True)  23.6 us
    unnamed x21, local copies, waits for them, and re-layouts  14.8 us
    all_gather x1, waiting for transfers between devices, local(): k_piece = lax.all_gather(arrived, 'row', axis=0, tiled=True)  9.23 us
    all_gather x1, blocking collectives, local(): lax.all_gather(lattice, 'row', axis=1, tiled=True)  5.19 us
    unnamed x1, blocking collectives  5.15 us
    unnamed x2, other arithmetic  5.07 us
    dot_general x1, local copies, waits for them, and re-layouts, local(): jnp.dot(factors, k_piece.reshape(fourier_amount, -1), preferred_element_t...  3.51 us
    convert_element_type x1, other arithmetic, local(): lattice_h = lattice_f.astype(jnp.bfloat16)  3.29 us
  transfers between devices with their start and end apart: 1, of which 1 were waited for; matrix products, arithmetic and copies ran while one was open for 2% of the time, Pallas kernels for 0%

commit v1 on v0

--- a/solution.py
+++ b/solution.py
@@ -54,7 +54,10 @@
     rotated = jnp.einsum(
         "kna,knb->kab", stacked, partner, preferred_element_type=jnp.float32
     ).astype(jnp.bfloat16)
-    arrived = lax.all_to_all(rotated, "ka", split_axis=1, concat_axis=0, tiled=True)
+    arrived = jnp.concatenate(
+        lax.all_to_all(jnp.stack(jnp.split(rotated, lax.axis_size("ka"), axis=1)), "ka", 0, 0),
+        axis=0,
+    )
     local_rows = arrived.shape[1]
     lattice_rows = lattice.shape[1]
     k_order = (

time: 96.8 us -> 89.6 us (0.926)
  other arithmetic: 12 us -> 7.64 us
  local copies, waits for them, and re-layouts: 20.9 us -> 17.9 us
    unnamed x2 -> x1, other arithmetic: 5.07 us -> 0.7 us
    unnamed x21 -> x24, local copies, waits for them, and re-layouts: 14.8 us -> 12.7 us
  transfers between devices with their start and end apart: 1 -> 1, of which waited for: 1 -> 1; matrix products, arithmetic and copies ran while one was open for 2% -> 3% of each run, Pallas kernels for 0% -> 0%
where the time goes in v1:
time: 89.6 us; the launch traced here: 89.2 us
  blocking collectives  34.1 us (38%)
  local copies, waits for them, and re-layouts  17.9 us (20%)
  between operations  14.9 us (17%)
  waiting for transfers between devices  9.25 us (10%)
  other arithmetic  7.64 us (9%)
  matrix products  5.37 us (6%)
    all_to_all x1, blocking collectives, local(): lax.all_to_all(jnp.stack(jnp.split(rotated, lax.axis_size('ka'), axis=1))...  23.7 us
    unnamed x24, local copies, waits for them, and re-layouts  12.7 us
    all_gather x1, waiting for transfers between devices, local(): k_piece = lax.all_gather(arrived, 'row', axis=0, tiled=True)  9.23 us
    all_gather x1, blocking collectives, local(): lax.all_gather(lattice, 'row', axis=1, tiled=True)  5.19 us
    unnamed x1, blocking collectives  5.15 us
    dot_general x1, local copies, waits for them, and re-layouts, local(): jnp.dot(factors, k_piece.reshape(fourier_amount, -1), preferred_element_t...  3.51 us
    convert_element_type x1, other arithmetic, local(): lattice_h = lattice_f.astype(jnp.bfloat16)  3.29 us
    dot_general x1, matrix products, local(): jnp.dot(factors, k_piece.reshape(fourier_amount, -1), preferred_element_t...  2.64 us
  transfers between devices with their start and end apart: 1, of which 1 were waited for; matrix products, arithmetic and copies ran while one was open for 3% of the time, Pallas kernels for 0%

profile of v1, /device:TPU:0, one launch (start us, length us, event | category | flops | bytes accessed | tf_op | source)
XLA Modules:
  0.0 89.2 jit_solution(6220958747442360841)
XLA Ops:
  7.2 0.7 reduce
  7.9 1.2 %multiply_convert_fusion = bf16[1,2,384,384]{3,2,1,0:T(8,128)(2,1)S(1)} fusion(bf16[1,2,384,384]{3,2,1,0:T(8,128)(2,1)} %param.6, f32[384]{0:T(512)S(1)} %reduce), kind=kLoop, calls=%fused_computation.23 | loop fusion | flops 884736 | bytes 1181184 | tf_op jit(solution)/shard_map/convert_element_type | solution.py:45
  9.2 1.3 %slice_bitcast_fusion.3 = (bf16[1,384,384]{2,1,0:T(8,128)(2,1)S(1)}, bf16[1,384,384]{2,1,0:T(8,128)(2,1)S(1)}, bf16[1,384,384]{2,1,0:T(8,128)(2,1)S(1)}, bf16[1,384,384]{2,1,0:T(8,128)(2,1)S(1)}) fusion(bf16[1,2,384,384]{3,2,1,0:T(8,128)(2,1)S(1)} %multiply_convert_fusion, bf16[1,2,384,384]{3,2,1,0:T(8,128)(2,1)} %param.6), kind=kLoop, calls=%fused_computation.28 | loop fusion | bytes 2359296 | tf_op jit(solution)/shard_map/squeeze | solution.py:49
  10.5 0.7 fusion.10
  11.3 23.7 %all_to_all.5 = bf16[8,1,48,768]{3,2,1,0:T(8,128)(2,1)} all-to-all(bf16[8,1,48,768]{3,2,1,0:T(8,128)(2,1)S(1)} %fusion.22), channel_id=1, replica_groups=mesh['ka'=8,'row'=4] {'ka'}, dimensions={0} | all-to-all | bytes 1179648 | tf_op jit(solution)/shard_map/all_to_all | solution.py:58
  35.0 5.2 %all-gather.1 = s32[4,64,3]{1,2,0:T(4,128)S(1)} all-gather(s32[1,64,3]{1,2,0:T(4,128)S(1)} %bitcast.117), channel_id=1, replica_groups=mesh['ka'=8,'row'=4] {'row'}, dimensions={0}, use_global_device_ids=true | all-gather | bytes 3840 | tf_op jit(solution)/shard_map/all_gather | solution.py:67
  40.4 0.1 copy.37
  40.7 0.1 cosine_convert_fusion.1
  41.0 0.6 dynamic-slice
  42.2 0.2 dynamic-update-slice
  42.5 5.2 %all-reduce = s32[256]{0:T(256)S(1)} all-reduce(s32[256]{0:T(256)S(1)} %dynamic-update-slice), channel_id=1, replica_groups=mesh['ka'=8,'row'=4] {'row'}, use_global_device_ids=true, to_apply=%add | all-reduce | flops 256 | bytes 2048
  48.0 0.3 fusion.36
  48.2 0.3 fusion.35
  48.5 9.2 %all-gather.4.cloned.1.call-done = bf16[32,1,48,768]{3,2,1,0:T(8,128)(2,1)} async-done(((bf16[8,1,48,768]{3,2,1,0:T(8,128)(2,1)}), bf16[32,1,48,768]{3,2,1,0:T(8,128)(2,1)}) %all-gather.4.cloned.1.call-update) | async-done | bytes 2359312 | tf_op jit(solution)/shard_map/all_gather | solution.py:89
  57.8 3.8 %copy.56 = bf16[4,8,48,768]{3,1,2,0:T(8,128)(2,1)} copy(bf16[4,8,48,768]{3,2,1,0:T(8,128)(2,1)} %bitcast.111) | data formatting | bytes 4718592
  61.6 3.5 %dot_general.23 = bf16[48,2,384,32]{2,1,0,3:T(2,128)(2,1)S(1)} reshape(bf16[36864,32]{0,1:T(8,128)(2,1)} %bitcast.110) | data formatting | bytes 4718592 | tf_op jit(solution)/shard_map/dot_general | solution.py:93
  65.1 1.5 %fusion.4 = f32[2,2,48,2,384]{4,1,3,2,0:T(2,128)S(1)} fusion(f32[2,2,32,1,1]{2,1,4,3,0:T(2,128)S(1)} %bitcast.116, bf16[48,2,384,32]{2,1,0,3:T(2,128)(2,1)S(1)} %dot_general.23), kind=kOutput, calls=%fused_computation.8 | convolution fusion | flops 56623104 | bytes 2949632 | tf_op jit(solution)/shard_map/dot_general | solution.py:96
  66.8 2.6 %fusion.6 = f32[2,64,48,2,384]{4,1,3,2,0:T(8,128)S(1)} fusion(bf16[48,2,384,32]{2,1,0,3:T(2,128)(2,1)S(1)} %dot_general.23, bf16[2,64,32,1,1]{1,0,2,4,3:T(2,128)(2,1)S(1)} %bitcast.112), kind=kOutput, calls=%fused_computation.10 | convolution fusion | flops 301989888 | bytes 21241856 | tf_op jit(solution)/shard_map/dot_general | solution.py:93
  69.5 0.8 fusion.1
  70.3 0.8 fusion.3
  71.0 0.1 pad_maximum_fusion
  71.2 0.7 copy.47
  71.9 3.3 %fusion = bf16[64,48,768]{2,0,1:T(8,128)(2,1)} fusion(f32[64,48,384]{2,0,1:T(8,128)S(1)} %fusion.1, f32[64,48,384]{2,0,1:T(8,128)S(1)} %fusion.3), kind=kLoop, calls=%fused_computation.1 | loop fusion | flops 7077888 | bytes 14155776 | tf_op jit(solution)/shard_map/convert_element_type | solution.py:106
  75.2 7.1 %copy.46 = bf16[64,48,768]{2,1,0:T(8,128)(2,1)} copy(bf16[64,48,768]{2,0,1:T(8,128)(2,1)} %fusion) | data formatting | bytes 9437184
  (39 shorter events, 1.2 us)
Async XLA Ops:
  7.2 40.5 %copy-start = (s32[3,8]{1,0:T(4,128)S(1)}, s32[3,8]{1,0:T(4,128)}, u32[]{:S(2)}) copy-start(s32[3,8]{1,0:T(4,128)} %param.11) | copy-start | bytes 292
  7.2 50.6 %all-gather.4.cloned.1.call-start = ((), (), s32[]{:S(2)}) async-start(), calls=%async_computation.1 | async-start | bytes 2949120 | tf_op jit(solution)/shard_map/all_gather | solution.py:89
  11.1 23.9 %copy-start.1 = (s32[3,64]{1,0:T(4,128)S(1)}, s32[3,64]{1,0:T(4,128)}, u32[]{:S(2)}) copy-start(s32[3,64]{1,0:T(4,128)} %param.9) | copy-start | bytes 2308
  11.1 29.2 %copy-start.2 = (s32[3,32]{1,0:T(4,128)S(1)}, s32[3,32]{1,0:T(4,128)}, u32[]{:S(2)}) copy-start(s32[3,32]{1,0:T(4,128)} %param.8) | copy-start | bytes 1156
  11.2 29.8 %copy-start.4 = (u32[32]{0:T(128)S(1)}, u32[32]{0:T(128)}, u32[]{:S(2)}) copy-start(u32[32]{0:T(128)} %constant.58) | copy-start | bytes 388
  11.2 31.0 %copy-start.3 = (s32[64]{0:T(128)S(1)}, s32[64]{0:T(128)}, u32[]{:S(2)}) copy-start(s32[64]{0:T(128)} %param.10) | copy-start | bytes 772
Sparse Core Ops, SparseCore 0:
  35.2 22.5 all-gather.3
